TPU v7x, 32 devices: a whole 2x2x4 slice. The times are simulated.
32 devices in a mesh: grp: 8 (over y, x, core), dom: 4 (over z).
Axes of the slice: x: 2, y: 2, z: 4, core: 2. Of those that a mesh axis runs over, the one named last changes fastest.
Arguments:
- surplus: float32 [128, 512, 512], P('grp', 'dom'), may hold values from -0.4 to 0.4
- block_ids: int32 [128, 512], P('grp', 'dom'), may hold values from 0 to 4095, as said below
- coef: int32 [128], P('grp'), may hold values from -4 to 6, as said below
Outputs:
- updated: float32 [128, 512, 512], P('grp', 'dom')
Inputs may be any that keep to these rules, and one draw needn't show every extreme that they name: `block_ids`: for each grid, the slots in columns d * 128 to (d + 1) * 128 - 1 hold 128 different numbers from d * 1024 to (d + 1) * 1024 - 1. `coef`: each coefficient is one of 1, -4, 6.
All inputs are finite; a program needn't handle non-finite values.
Results may differ from a plain program's by a relative error of at most 0.000071.
Values sent between devices are 32-bit elements; how exact they have to be, the bound alone decides.
A program may use at most 64 MiB of HBM per device.

v0:
```python
import jax
import jax.numpy as jnp
from jax import lax
from jax.sharding import PartitionSpec as P

NBD = 1024


def local(surplus, block_ids, coef):
    offset = lax.axis_index("dom") * NBD
    local_ids = block_ids - offset
    columns = lax.broadcasted_iota(jnp.int32, (1, 1, NBD), 2)
    onehot = (local_ids[:, :, None] == columns).astype(jnp.float32)
    scaled = surplus * coef.astype(jnp.float32)[:, None, None]
    partial_sum = jnp.einsum("gkn,gkb->nb", onehot, scaled, precision=lax.Precision.HIGHEST)
    combined = lax.psum(partial_sum, "grp")
    return jnp.einsum("gkn,nb->gkb", onehot, combined, precision=lax.Precision.HIGHEST)


def solution(mesh):
    return jax.shard_map(
        local,
        mesh=mesh,
        in_specs=(P("grp", "dom", None), P("grp", "dom"), P("grp")),
        out_specs=P("grp", "dom", None),
        check_vma=False,
    )
```

profile of v0, /device:TPU:0, one launch (start us, length us, event | category | flops | bytes accessed | tf_op | source)
XLA Modules:
  0.0 106.6 jit_solution(6642148042508687133)
XLA Ops:
  6.5 0.0 all-reduce.2.cloned.1.call-start
  6.5 0.7 convert_element_type.4
  7.2 0.7 broadcast_subtract_fusion
  7.9 16.8 %fusion.7 = f32[1024,512]{1,0:T(8,128)} fusion(f32[16,128,512]{2,1,0:T(8,128)} %param.3, f32[16]{0:T(128)S(1)} %convert_element_type.4, s32[16,128]{1,0:T(8,128)S(1)} %broadcast_subtract_fusion), kind=kOutput, calls=%fused_computation.8 | convolution fusion | flops 12888047616 | bytes 6299712 | tf_op jit(solution)/shard_map/gkn,gkb->nb/dot_general | solution.py:15
  24.7 0.0 all-reduce.2.cloned.1.call-update
  24.7 64.6 %all-reduce.2.cloned.1.call-done = f32[1024,512]{1,0:T(8,128)} async-done(((f32[1024,512]{1,0:T(8,128)}), f32[1024,512]{1,0:T(8,128)}) %all-reduce.2.cloned.1.call-update) | async-done | bytes 2097168 | tf_op jit(solution)/shard_map/psum | solution.py:16
  89.3 10.4 %fusion = f32[16,128,512]{2,1,0:T(8,128)} fusion(s32[16,128]{1,0:T(8,128)S(1)} %broadcast_subtract_fusion, f32[1024,512]{1,0:T(8,128)} %all-reduce.2.cloned.1.call-done), kind=kOutput, calls=%fused_computation.1 | convolution fusion | flops 12886999040 | bytes 6299648 | tf_op jit(solution)/shard_map/gkn,nb->gkb/dot_general | solution.py:17
Async XLA Ops:
  6.5 82.8 %all-reduce.2.cloned.1.call-start = ((), (), s32[]{:S(2)}) async-start(), calls=%async_computation | async-start | bytes 4194304 | tf_op jit(solution)/shard_map/psum | solution.py:16
Sparse Core Ops, SparseCore 0:
  24.8 64.4 all-reduce.1
where the time goes:
time: 107 us
  waiting for transfers between devices  64.7 us (60%)
  matrix products  27.2 us (25%)
  between operations  13.4 us (13%)
  other arithmetic  1.36 us (1%)
    psum x1, waiting for transfers between devices, local(): combined = lax.psum(partial_sum, 'grp')  64.6 us
    dot_general x1, matrix products, local(): jnp.einsum('gkn,gkb->nb', onehot, scaled, precision=lax.Precision.HIGHEST)  16.8 us
    dot_general x1, matrix products, local(): jnp.einsum('gkn,nb->gkb', onehot, combined, precision=lax.Precision.HIGHEST)  10.4 us
  transfers between devices with their start and end apart: 1, of which 1 were waited for; matrix products, arithmetic and copies ran while one was open for 0% of the time, Pallas kernels for 0%

commit v1 on v0

--- a/solution.py
+++ b/solution.py
@@ -13,7 +13,9 @@
     onehot = (local_ids[:, :, None] == columns).astype(jnp.float32)
     scaled = surplus * coef.astype(jnp.float32)[:, None, None]
     partial_sum = jnp.einsum("gkn,gkb->nb", onehot, scaled, precision=lax.Precision.HIGHEST)
-    combined = lax.psum(partial_sum, "grp")
+    combined = partial_sum
+    for hop in (1, 2, 4):
+        combined = combined + lax.ppermute(combined, "grp", [(dev, dev ^ hop) for dev in range(8)])
     return jnp.einsum("gkn,nb->gkb", onehot, combined, precision=lax.Precision.HIGHEST)
 
 

time: 107 us -> 128 us (1.20)
  waiting for transfers between devices: 64.7 us -> 95 us
  between operations: 13.4 us -> 0.02 us
  starting transfers between devices: 0.01 us -> 5.3 us
  matrix products: 27.2 us -> 24.7 us
    ppermute x0 -> x3, waiting for transfers between devices: none -> 95 us  [local(): lax.ppermute(combined, 'grp', [(dev, dev ^ hop) for dev in range(8)])]
    psum x1 -> x0, waiting for transfers between devices: 64.6 us -> none  [local(): combined = lax.psum(partial_sum, 'grp')]
    ppermute x0 -> x3, starting transfers between devices: none -> 5.3 us  [local(): lax.ppermute(combined, 'grp', [(dev, dev ^ hop) for dev in range(8)])]
    dot_general x1, matrix products: 10.4 us -> 8.48 us  [local(): jnp.einsum('gkn,nb->gkb', onehot, combined, precision=lax.Precision.HIGHEST)]
  transfers between devices with their start and end apart: 1 -> 3, of which waited for: 1 -> 3; matrix products, arithmetic and copies ran while one was open for 0% -> 0% of each run, Pallas kernels for 0% -> 0%
where the time goes in v1:
time: 128 us; the launch traced here: 127 us
  waiting for transfers between devices  95 us (74%)
  matrix products  24.7 us (19%)
  starting transfers between devices  5.3 us (4%)
  other arithmetic  2.31 us (2%)
    ppermute x3, waiting for transfers between devices, local(): lax.ppermute(combined, 'grp', [(dev, dev ^ hop) for dev in range(8)])  95 us
    dot_general x1, matrix products, local(): jnp.einsum('gkn,gkb->nb', onehot, scaled, precision=lax.Precision.HIGHEST)  16.3 us
    dot_general x1, matrix products, local(): jnp.einsum('gkn,nb->gkb', onehot, combined, precision=lax.Precision.HIGHEST)  8.48 us
    ppermute x3, starting transfers between devices, local(): lax.ppermute(combined, 'grp', [(dev, dev ^ hop) for dev in range(8)])  5.3 us
  transfers between devices with their start and end apart: 3, of which 3 were waited for; matrix products, arithmetic and copies ran while one was open for 0% of the time, Pallas kernels for 0%

profile of v1, /device:TPU:0, one launch (start us, length us, event | category | flops | bytes accessed | tf_op | source)
XLA Modules:
  0.0 127.4 jit_solution(6808424795790659561)
XLA Ops:
  0.0 0.7 convert_element_type.4
  0.7 0.7 broadcast_subtract_fusion
  1.4 16.3 %fusion.8 = f32[1024,512]{1,0:T(8,128)S(1)} fusion(f32[16,128,512]{2,1,0:T(8,128)} %param.3, f32[16]{0:T(128)S(1)} %convert_element_type.4, s32[16,128]{1,0:T(8,128)S(1)} %broadcast_subtract_fusion), kind=kOutput, calls=%fused_computation.9 | convolution fusion | flops 12888047616 | bytes 6299712 | tf_op jit(solution)/shard_map/gkn,gkb->nb/dot_general | solution.py:15
  17.6 0.6 collective-permute-start
  18.2 3.8 %collective-permute-done = f32[1024,512]{1,0:T(8,128)S(1)} collective-permute-done((f32[1024,512]{1,0:T(8,128)S(1)}, f32[1024,512]{1,0:T(8,128)S(1)}, u32[]{:S(2)}, u32[]{:S(2)}) %collective-permute-start) | collective-permute-done | bytes 2097184 | tf_op jit(solution)/shard_map/ppermute | solution.py:18
  22.0 0.5 add.9
  22.4 2.9 %collective-permute-start.1 = (f32[1024,512]{1,0:T(8,128)S(1)}, f32[1024,512]{1,0:T(8,128)S(1)}, u32[]{:S(2)}, u32[]{:S(2)}) collective-permute-start(f32[1024,512]{1,0:T(8,128)S(1)} %add.9), channel_id=1, source_target_pairs={{0,8},{4,12},{8,0},{12,4},{16,24},{20,28},{24,16},{28,20},{1,9},{5... | collective-permute-start | bytes 6291464 | tf_op jit(solution)/shard_map/ppermute | solution.py:18
  25.4 45.9 %collective-permute-done.1 = f32[1024,512]{1,0:T(8,128)S(1)} collective-permute-done((f32[1024,512]{1,0:T(8,128)S(1)}, f32[1024,512]{1,0:T(8,128)S(1)}, u32[]{:S(2)}, u32[]{:S(2)}) %collective-permute-start.1) | collective-permute-done | bytes 2097184 | tf_op jit(solution)/shard_map/ppermute | solution.py:18
  71.3 0.5 add.10
  71.8 1.8 %collective-permute-start.2 = (f32[1024,512]{1,0:T(8,128)S(1)}, f32[1024,512]{1,0:T(8,128)S(1)}, u32[]{:S(2)}, u32[]{:S(2)}) collective-permute-start(f32[1024,512]{1,0:T(8,128)S(1)} %add.10), channel_id=1, source_target_pairs={{0,16},{4,20},{8,24},{12,28},{16,0},{20,4},{24,8},{28,12},{1,17},{... | collective-permute-start | bytes 6291464 | tf_op jit(solution)/shard_map/ppermute | solution.py:18
  73.6 45.3 %collective-permute-done.2 = f32[1024,512]{1,0:T(8,128)S(1)} collective-permute-done((f32[1024,512]{1,0:T(8,128)S(1)}, f32[1024,512]{1,0:T(8,128)S(1)}, u32[]{:S(2)}, u32[]{:S(2)}) %collective-permute-start.2) | collective-permute-done | bytes 2097184 | tf_op jit(solution)/shard_map/ppermute | solution.py:18
  118.9 8.5 %fusion = f32[16,128,512]{2,1,0:T(8,128)} fusion(s32[16,128]{1,0:T(8,128)S(1)} %broadcast_subtract_fusion, f32[1024,512]{1,0:T(8,128)S(1)} %add.10, f32[1024,512]{1,0:T(8,128)S(1)} %collective-permute-done.2), kind=kOutput, calls=%fused_computation.1 | convolution fusion | flops 12887523328 | bytes 8396800 | tf_op jit(solution)/shard_map/gkn,nb->gkb/dot_general | solution.py:19
Async XLA Ops:
  17.6 4.3 %collective-permute-start = (f32[1024,512]{1,0:T(8,128)S(1)}, f32[1024,512]{1,0:T(8,128)S(1)}, u32[]{:S(2)}, u32[]{:S(2)}) collective-permute-start(f32[1024,512]{1,0:T(8,128)S(1)} %fusion.8), channel_id=1, source_target_pairs={{0,4},{4,0},{8,12},{12,8},{16,20},{20,16},{24,28},{28,24},{1,5},{5... | collective-permute-start | bytes 6291464 | tf_op jit(solution)/shard_map/ppermute | solution.py:18
  22.4 48.8 %collective-permute-start.1 = (f32[1024,512]{1,0:T(8,128)S(1)}, f32[1024,512]{1,0:T(8,128)S(1)}, u32[]{:S(2)}, u32[]{:S(2)}) collective-permute-start(f32[1024,512]{1,0:T(8,128)S(1)} %add.9), channel_id=1, source_target_pairs={{0,8},{4,12},{8,0},{12,4},{16,24},{20,28},{24,16},{28,20},{1,9},{5... | collective-permute-start | bytes 6291464 | tf_op jit(solution)/shard_map/ppermute | solution.py:18
  71.8 47.2 %collective-permute-start.2 = (f32[1024,512]{1,0:T(8,128)S(1)}, f32[1024,512]{1,0:T(8,128)S(1)}, u32[]{:S(2)}, u32[]{:S(2)}) collective-permute-start(f32[1024,512]{1,0:T(8,128)S(1)} %add.10), channel_id=1, source_target_pairs={{0,16},{4,20},{8,24},{12,28},{16,0},{20,4},{24,8},{28,12},{1,17},{... | collective-permute-start | bytes 6291464 | tf_op jit(solution)/shard_map/ppermute | solution.py:18
